TPU v7x, 32 devices: a whole 2x2x4 slice. The times are simulated.
32 devices in a mesh: chan: 4 (over y, x), slab: 8 (over z, core).
Axes of the slice: x: 2, y: 2, z: 4, core: 2. Of those that a mesh axis runs over, the one named last changes fastest.
Arguments:
- taylor_models: float32 [2, 2048, 2048], P(None, 'slab', 'chan'), may hold values from -6 to 6
- gridded_vis: bfloat16 [4, 2, 2048, 2048], P('chan', None, 'slab'), may hold values from -6 to 6
- uv_weight: bfloat16 [4, 2048, 2048], P('chan', 'slab'), may hold values from 0 to 2
- freq_ratio: float32 [4], P('chan'), may hold values from 0.6 to 1.4
- robust_scale: float32 [4], P('chan'), may hold values from 0.25 to 4
Outputs:
- taylor_residual: float32 [2, 2048, 2048], P(None, 'slab', 'chan')
All inputs are finite; a program needn't handle non-finite values.
Results may differ from a plain program's by a relative error of at most 0.0003.
Values sent between devices are 32-bit elements; how exact they have to be, the bound alone decides.
A program may use at most 64 MiB of HBM per device.

v0:
```python
import functools
import math

import jax
import jax.numpy as jnp
import numpy as np
from jax import lax
from jax.experimental import pallas as pl
from jax.experimental.pallas import tpu as pltpu
from jax.sharding import PartitionSpec as P

MESH = pl.DeviceIdType.MESH
TERMS = 2
RADIX = 16
LANES = 128
PARTS = 4


def fine_tables():
    points = RADIX * LANES
    j = np.arange(RADIX)[:, None, None]
    k = np.arange(LANES)[None, :, None]
    a = np.arange(LANES)[None, None, :]
    angle = 2.0 * np.pi / points * ((a * (RADIX * k + j)) % points)
    cos, sin = np.cos(angle), -np.sin(angle)
    full = np.concatenate(
        [np.concatenate([cos, -sin], axis=2), np.concatenate([sin, cos], axis=2)], axis=1
    ).astype(np.float32)
    back = np.ascontiguousarray(full.transpose(0, 2, 1))

    def halves(table):
        high = table.astype(jnp.bfloat16)
        low = (table - high.astype(np.float32)).astype(jnp.bfloat16)
        return np.stack([high, low])

    return halves(full), halves(back)


def swap_table(outer, inner):
    size = outer * inner
    table = np.zeros((size, size), np.float32)
    rows = np.arange(size)
    table[rows, (rows % inner) * outer + rows // inner] = 1.0
    return table.astype(jnp.bfloat16)


def plus(a, b):
    if a is None:
        return b
    return a if b is None else a + b


def minus(a, b):
    if b is None:
        return a
    return -b if a is None else a - b


def times(a, s):
    return None if a is None or s == 0.0 else a * s


def cadd(a, b):
    return plus(a[0], b[0]), plus(a[1], b[1])


def csub(a, b):
    return minus(a[0], b[0]), minus(a[1], b[1])


def turn(a, sign):
    if sign > 0:
        return minus(None, a[1]) if a[1] is not None else None, a[0]
    return a[1], minus(None, a[0]) if a[0] is not None else None


def ctwist(a, step, sign):
    step %= RADIX
    if step == 0:
        return a
    if step == 4:
        return turn(a, sign)
    c, s = math.cos(2 * math.pi * step / RADIX), sign * math.sin(2 * math.pi * step / RADIX)
    if step % 8 == 2:
        return times(minus(a[0], times(a[1], sign)), c), times(plus(times(a[0], sign), a[1]), c)
    return minus(times(a[0], c), times(a[1], s)), plus(times(a[0], s), times(a[1], c))


def four(a, b, c, d, sign):
    t0, t1, t2, t3 = cadd(a, c), csub(a, c), cadd(b, d), turn(csub(b, d), sign)
    return cadd(t0, t2), cadd(t1, t3), csub(t0, t2), csub(t1, t3)


def sixteen(x, sign):
    mid = [four(x[n], x[4 + n], x[8 + n], x[12 + n], sign) for n in range(4)]
    out = [None] * RADIX
    for k in range(4):
        tw = [ctwist(mid[n][k], n * k, sign) for n in range(4)]
        for q, y in enumerate(four(*tw, sign)):
            out[k + 4 * q] = y
    return out


def fine(table_ref, j, x):
    high = x.astype(jnp.bfloat16)
    low = (x - high.astype(jnp.float32)).astype(jnp.bfloat16)
    t_high, t_low = table_ref[0, j], table_ref[1, j]
    dot = functools.partial(jnp.dot, preferred_element_type=jnp.float32)
    return dot(t_high, high) + (dot(t_high, low) + dot(t_low, high))


def al8(i):
    return pl.multiple_of(i, 8)


def kernel(
    C, S,
    x_hbm, vis_hbm, wt_hbm, freq_ref, rob_ref, fwd_hbm, bwd_hbm, pu_hbm, pv_hbm,
    out_hbm,
    xr, xt, y_s, z_s, w_s, rs, rr, ms, mr, bs, br, ts, tr, x_s, zz_s, os_, fwd, bwd, pu, pv,
    raw, vt, offs,
    load_sem, x_send, x_recv, x_own, o_send, o_recv, o_own, f_send, f_recv,
    r_send, r_recv, r_own, m_send, m_recv, m_own, b_send, b_recv, b_own, t_send, t_recv, t_own,
):
    H = rs.shape[0]
    sub = x_hbm.shape[1] // C
    rows, cols = x_hbm.shape[1], x_hbm.shape[2]
    jper = RADIX // H
    kl = LANES // S
    piece = sub // PARTS
    scale = 1.0 / (RADIX * LANES)
    c_me, s_me = lax.axis_index("chan"), lax.axis_index("slab")
    chan_peers = [lax.rem(c_me + d, C) for d in range(1, C)]
    slab_peers = [lax.rem(s_me + d, S) for d in range(1, S)]

    def load(n):
        source, target = (
            (fwd_hbm, fwd),
            (vis_hbm.at[0], raw.at[pl.ds(0, 2)]),
            (wt_hbm, raw.at[pl.ds(2, 1)]),
            (pu_hbm, pu),
            (pv_hbm, pv),
            (bwd_hbm, bwd),
        )[n]
        return pltpu.make_async_copy(source, target, load_sem.at[n])

    def remote(src, dst, send, recv, **where):
        pltpu.make_async_remote_copy(
            src_ref=src, dst_ref=dst, send_sem=send, recv_sem=recv,
            device_id=where, device_id_type=MESH,
        ).start()

    def own(src, dst, sem):
        pltpu.make_async_copy(src, dst, sem).start()

    def landed(ref, sem):
        pltpu.make_async_copy(ref, ref, sem).wait()

    barrier = pltpu.get_barrier_semaphore()
    own(x_hbm.at[:, pl.ds(al8(sub * c_me), sub), :], xr.at[c_me], x_own)
    for n in range(6):
        load(n).start()
    for c in chan_peers:
        pl.semaphore_signal(barrier, inc=1, device_id={"chan": c}, device_id_type=MESH)
    for s in slab_peers:
        pl.semaphore_signal(barrier, inc=1, device_id={"slab": s}, device_id_type=MESH)
    pl.semaphore_wait(barrier, C + S - 2)

    for c in chan_peers:
        remote(
            x_hbm.at[:, pl.ds(al8(sub * c), sub), :], xr.at[c_me], x_send, x_recv, chan=c
        )
    own(freq_ref, offs.at[c_me], o_own)
    for c in chan_peers:
        remote(freq_ref, offs.at[c_me], f_send, f_recv, chan=c)

    def prep():
        for n in range(1, 5):
            load(n).wait()

        def body(n, carry):
            which, m = n // 8, n % 8
            block = raw[which, :, pl.ds(pl.multiple_of(m * 256, 256), 256)]
            turned = jnp.dot(pu[...], block, preferred_element_type=jnp.float32)
            flipped = lax.dot_general(
                pv[...], turned.astype(jnp.bfloat16), (((1,), (1,)), ((), ())),
                preferred_element_type=jnp.float32,
            ).astype(jnp.bfloat16)
            for h in range(H):
                for j in range(RADIX):
                    vt[which, h, j, pl.ds(pl.multiple_of(16 * m, 16), 16), :] = flipped[
                        16 * j : 16 * j + 16, LANES * h : LANES * (h + 1)
                    ]
            return carry

        lax.fori_loop(0, 24, body, 0)

    def rows_in():
        landed(xr.at[pl.ds(0, C - 1)], x_recv)
        landed(xr.at[0], x_own)
        load(0).wait()
        per = cols // LANES
        for b in range(RADIX):
            tile = xr[b // per, :, :, LANES * (b % per) : LANES * (b % per + 1)]
            xt[b] = tile.reshape(TERMS * sub, LANES).T

        def body(n, carry):
            at = al8(8 * n)
            out = sixteen([(xt[b, pl.ds(at, 8), :], None) for b in range(RADIX)], -1)
            for j in range(RADIX):
                for part in range(2):
                    value = out[j][part]
                    if value is None:
                        value = jnp.zeros((8, LANES), jnp.float32)
                    y_s[j, pl.ds(al8(part * LANES + at), 8), :] = value
            return carry

        lax.fori_loop(0, LANES // 8, body, 0)

    def rows_out(h):
        def body(jl, carry):
            z = fine(fwd, jper * h + jl, y_s[jper * h + jl])
            for s in range(S):
                for part in range(2):
                    w_s[s, part, pl.ds(al8(kl * jl), kl), :] = z[
                        part * LANES + kl * s : part * LANES + kl * (s + 1), :
                    ]
            return carry

        lax.fori_loop(0, jper, body, 0)

        def flip(s, carry):
            for part in range(2):
                rs[h, s, part] = w_s[s, part].T.reshape(TERMS, sub, LANES)
            return carry

        lax.fori_loop(0, S, flip, 0)
        for q in range(PARTS):
            span = pl.ds(q * piece, piece)
            own(rs.at[h, s_me, :, :, span, :], rr.at[h, s_me, :, :, span, :], r_own.at[h, q])
            for s in slab_peers:
                remote(
                    rs.at[h, s, :, :, span, :], rr.at[h, s_me, :, :, span, :],
                    r_send, r_recv.at[h, q], slab=s,
                )

    def mix(h, q):
        span = pl.ds(q * piece, piece)
        landed(rr.at[h, pl.ds(0, S - 1), :, :, span, :], r_recv.at[h, q])
        landed(rr.at[h, 0, :, :, span, :], r_own.at[h, q])

        def body(s, carry):
            base = rr[h, s, :, 0, span, :] * scale
            slope = rr[h, s, :, 1, span, :] * scale
            for c in range(C):
                offset = offs[c, 0:1, :] - 1.0
                ms[h, c, :, s, span, :] = base + offset[None] * slope
            return carry

        lax.fori_loop(0, S, body, 0)
        there = pl.ds(al8(sub * c_me + q * piece), piece)
        own(ms.at[h, c_me, :, :, span, :], mr.at[h, :, :, there, :], m_own.at[h])
        for c in chan_peers:
            remote(
                ms.at[h, c, :, :, span, :], mr.at[h, :, :, there, :],
                m_send, m_recv.at[h], chan=c,
            )

    def column_in(h):
        landed(ms.at[h, pl.ds(0, C - 1)], m_recv.at[h])
        landed(ms.at[h, 0], m_own.at[h])

        def body(n, carry):
            at = 8 * n
            x = []
            for b in range(RADIX):
                s, row = LANES * b // rows, LANES * b % rows
                x.append(tuple(mr[h, part, s, pl.ds(al8(row + at), 8), :] for part in range(2)))
            out = sixteen(x, -1)
            for j in range(RADIX):
                for part in range(2):
                    y_s[j, pl.ds(al8(part * LANES + at), 8), :] = out[j][part]
            return carry

        lax.fori_loop(0, LANES // 8, body, 0)

    def column_mid(h):
        def body(j, carry):
            z = fine(fwd, j, y_s[j])
            weight = vt[2, h, j].astype(jnp.float32)
            real = vt[0, h, j].astype(jnp.float32) - weight * z[:LANES]
            imag = vt[1, h, j].astype(jnp.float32) - weight * z[LANES:]
            robust = 1.0 / (1.0 + rob_ref[0] * (real * real + imag * imag))
            z_s[j] = fine(bwd, j, jnp.concatenate([robust * real, robust * imag], axis=0))
            return carry

        lax.fori_loop(0, RADIX, body, 0)

    def column_out(h, q):
        per = piece // 8

        def body(n, carry):
            at = sub * (n // per) + q * piece + 8 * (n % per)
            out = sixteen(
                [tuple(z_s[j, pl.ds(al8(part * LANES + at), 8), :] for part in range(2)) for j in range(RADIX)],
                1,
            )
            for b in range(RADIX):
                s, row = LANES * b // rows, LANES * b % rows
                for part in range(2):
                    bs[h, part, s, pl.ds(al8(row + at), 8), :] = out[b][part]
            return carry

        lax.fori_loop(0, LANES // sub * per, body, 0)
        span = pl.ds(q * piece, piece)
        here = lambda c: pl.ds(al8(sub * c + q * piece), piece)
        own(bs.at[h, :, :, here(c_me), :], br.at[h, c_me, :, :, span, :], b_own.at[h, q])
        for c in chan_peers:
            remote(
                bs.at[h, :, :, here(c), :], br.at[h, c_me, :, :, span, :],
                b_send, b_recv.at[h, q], chan=c,
            )

    def gather(h, q):
        span = pl.ds(q * piece, piece)
        landed(br.at[h, pl.ds(0, C - 1), :, :, span, :], b_recv.at[h, q])
        landed(br.at[h, 0, :, :, span, :], b_own.at[h, q])

        def body(s, carry):
            base, slope = None, None
            for c in range(C):
                offset = (offs[c, 0:1, :] - 1.0)[None]
                value = br[h, c, :, s, span, :]
                base = value if base is None else base + value
                slope = offset * value if slope is None else slope + offset * value
            ts[h, s, :, 0, span, :] = base * scale
            ts[h, s, :, 1, span, :] = slope * scale
            return carry

        lax.fori_loop(0, S, body, 0)
        own(ts.at[h, s_me, :, :, span, :], tr.at[h, s_me, :, :, span, :], t_own.at[h])
        for s in slab_peers:
            remote(
                ts.at[h, s, :, :, span, :], tr.at[h, s_me, :, :, span, :],
                t_send, t_recv.at[h], slab=s,
            )

    def back_in(h):
        landed(tr.at[h, pl.ds(0, S - 1)], t_recv.at[h])
        landed(tr.at[h, 0], t_own.at[h])

        def flip(s, carry):
            for part in range(2):
                tile = tr[h, s, part].reshape(TERMS * sub, LANES).T
                for jl in range(jper):
                    x_s[jper * h + jl, pl.ds(al8(part * LANES + kl * s), kl), :] = tile[
                        kl * jl : kl * (jl + 1), :
                    ]
            return carry

        lax.fori_loop(0, S, flip, 0)

        def body(jl, carry):
            zz_s[jper * h + jl] = fine(bwd, jper * h + jl, x_s[jper * h + jl])
            return carry

        lax.fori_loop(0, jper, body, 0)

    def back_out():
        def body(n, carry):
            at = 8 * n
            out = sixteen(
                [tuple(zz_s[j, pl.ds(al8(part * LANES + at), 8), :] for part in range(2)) for j in range(RADIX)],
                1,
            )
            for b in range(RADIX):
                xt[b, pl.ds(al8(at), 8), :] = out[b][0]
            return carry

        lax.fori_loop(0, LANES // 8, body, 0)
        per = cols // LANES
        for b in range(RADIX):
            os_[b // per, :, :, LANES * (b % per) : LANES * (b % per + 1)] = xt[b].T.reshape(
                TERMS, sub, LANES
            )
        there = pl.ds(al8(sub * c_me), sub)
        for c in chan_peers:
            remote(os_.at[c], out_hbm.at[:, there, :], o_send, o_recv, chan=c)
        own(os_.at[c_me], out_hbm.at[:, there, :], o_own)

    prep()
    landed(offs.at[pl.ds(0, C - 1)], f_recv)
    landed(offs.at[0], o_own)
    rows_in()
    for h in range(H):
        rows_out(h)
    for h in range(H):
        for q in range(PARTS):
            mix(h, q)
    load(5).wait()
    for h in range(H):
        column_in(h)
        column_mid(h)
        for q in range(PARTS):
            column_out(h, q)
    for h in range(H):
        for q in range(PARTS):
            gather(h, q)
    for h in range(H):
        back_in(h)
    back_out()

    landed(xr.at[pl.ds(0, C - 1)], x_send)
    landed(offs.at[pl.ds(0, C - 1)], f_send)
    landed(rs.at[:, pl.ds(0, S - 1)], r_send)
    landed(ms.at[:, pl.ds(0, C - 1)], m_send)
    landed(br.at[:, pl.ds(0, C - 1)], b_send)
    landed(ts.at[:, pl.ds(0, S - 1)], t_send)
    landed(os_.at[pl.ds(0, C - 1)], o_send)
    landed(os_.at[pl.ds(0, C - 1)], o_recv)
    landed(os_.at[0], o_own)


def tiled(taylor_models, gridded_vis, uv_weight, freq_ratio, robust_scale):
    C, S = lax.axis_size("chan"), lax.axis_size("slab")
    terms, rows, cols = taylor_models.shape
    sub = rows // C
    U = gridded_vis.shape[2]
    H = U // LANES
    fwd, bwd = fine_tables()
    pu, pv = swap_table(RADIX, U // RADIX), swap_table(RADIX, 16)
    freq = jnp.broadcast_to(freq_ratio[:, None], (8, LANES))
    f32, bf16 = jnp.float32, jnp.bfloat16
    stage = (RADIX, 2 * LANES, LANES)
    slabbed = (H, S, 2, terms, sub, LANES)
    chanbed = (H, C, 2, S, sub, LANES)
    natural = (H, 2, S, rows, LANES)
    V = lambda shape, dtype=f32: pltpu.VMEM(shape, dtype)
    D = pltpu.SemaphoreType.DMA
    anywhere = pl.BlockSpec(memory_space=pl.ANY)
    return pl.pallas_call(
        functools.partial(kernel, C, S),
        out_shape=jax.ShapeDtypeStruct(taylor_models.shape, f32),
        in_specs=[
            anywhere, anywhere, anywhere,
            pl.BlockSpec(memory_space=pltpu.VMEM), pl.BlockSpec(memory_space=pltpu.SMEM),
            anywhere, anywhere, anywhere, anywhere,
        ],
        out_specs=anywhere,
        scratch_shapes=[
            V((C, terms, sub, cols)), V((RADIX, LANES, LANES)), V(stage), V(stage),
            V((S, 2, LANES, LANES)), V(slabbed), V(slabbed), V(chanbed), V(natural),
            V(natural), V(chanbed), V(slabbed), V(slabbed), V(stage), V(stage),
            V((C, terms, sub, cols)), V(fwd.shape, bf16), V(bwd.shape, bf16),
            V(pu.shape, bf16), V(pv.shape, bf16),
            V((3, U, RADIX * LANES), bf16), V((3, H, RADIX, LANES, LANES), bf16),
            V((C, 8, LANES)),
            D((6,)), D(()), D(()), D(()), D(()), D(()), D(()), D(()), D(()),
            D(()), D((H, PARTS)), D((H, PARTS)),
            D(()), D((H,)), D((H,)),
            D(()), D((H, PARTS)), D((H, PARTS)),
            D(()), D((H,)), D((H,)),
        ],
        compiler_params=pltpu.CompilerParams(
            collective_id=0, has_side_effects=True, vmem_limit_bytes=63 * 1024 * 1024
        ),
    )(taylor_models, gridded_vis, uv_weight, freq, robust_scale, fwd, bwd, pu, pv)


HIGHEST = lax.Precision.HIGH


def dft_table(points, direction):
    steps_all = jnp.arange(points, dtype=jnp.int32)
    product = steps_all[:, None] * steps_all[None, :] % points
    angles = product.astype(jnp.float32) * (2.0 * math.pi / points)
    return (jnp.cos(angles), direction * jnp.sin(angles))


def twiddle_table(outer_points, inner_points, direction):
    outer_steps = jnp.arange(outer_points, dtype=jnp.int32)
    inner_steps = jnp.arange(inner_points, dtype=jnp.int32)
    overall = outer_points * inner_points
    product = outer_steps[:, None] * inner_steps[None, :] % overall
    angles = product.astype(jnp.float32) * (2.0 * math.pi / overall)
    return (jnp.cos(angles), direction * jnp.sin(angles))


def complex_product(formula, left_real, left_imag, table_real, table_imag):
    out_real = jnp.einsum(formula, left_real, table_real, precision=HIGHEST) - jnp.einsum(
        formula, left_imag, table_imag, precision=HIGHEST
    )
    out_imag = jnp.einsum(formula, left_real, table_imag, precision=HIGHEST) + jnp.einsum(
        formula, left_imag, table_real, precision=HIGHEST
    )
    return (out_real, out_imag)


def rotate(left_real, left_imag, table_real, table_imag):
    return (
        left_real * table_real - left_imag * table_imag,
        left_real * table_imag + left_imag * table_real,
    )


def general(taylor_models, gridded_vis, uv_weight, freq_ratio, robust_scale):
    inner_count = 128
    PIX = taylor_models.shape[2] * lax.axis_size("chan")
    outer_count = PIX // inner_count
    chans = lax.axis_size("chan")
    slabs = lax.axis_size("slab")
    rows = taylor_models.shape[1]
    cols = taylor_models.shape[2]
    sub = rows // chans
    col_count = PIX // slabs
    outer_cos, outer_sin = dft_table(outer_count, -1.0)
    inner_cos, inner_sin = dft_table(inner_count, -1.0)
    twist_cos, twist_sin = twiddle_table(outer_count, inner_count, -1.0)
    offsets = lax.all_gather(freq_ratio, "chan", axis=0, tiled=True) - 1.0

    pieces = taylor_models.reshape(TERMS, chans, sub, cols).transpose(1, 0, 2, 3)
    pieces = lax.all_to_all(pieces, "chan", split_axis=0, concat_axis=0, tiled=True)
    layered = pieces.transpose(1, 2, 0, 3).reshape(TERMS * sub, outer_count, inner_count)
    part_real = jnp.einsum("yba,jb->yja", layered, outer_cos, precision=HIGHEST)
    part_imag = jnp.einsum("yba,jb->yja", layered, outer_sin, precision=HIGHEST)
    turned_real, turned_imag = rotate(part_real, part_imag, twist_cos, twist_sin)
    spec_real, spec_imag = complex_product(
        "yja,ka->kjy", turned_real, turned_imag, inner_cos, inner_sin
    )
    outgoing = jnp.stack(
        [
            spec_real.reshape(slabs, col_count, TERMS * sub),
            spec_imag.reshape(slabs, col_count, TERMS * sub),
        ],
        axis=1,
    )
    arrived = lax.all_to_all(outgoing, "slab", split_axis=0, concat_axis=0, tiled=True)
    arrived = arrived.reshape(slabs, 2, col_count, TERMS, sub)
    arrived = arrived.transpose(3, 1, 2, 0, 4).reshape(TERMS, 2, col_count, slabs * sub)
    mixed = arrived[0][None] + offsets[:, None, None, None] * arrived[1][None]
    mixed = lax.all_to_all(mixed, "chan", split_axis=0, concat_axis=0, tiled=True)
    columns = mixed.reshape(chans, 2, col_count, slabs, sub).transpose(1, 2, 3, 0, 4)
    layered_cols = columns.reshape(2, col_count, outer_count, inner_count)
    part_real, part_imag = complex_product(
        "uba,jb->uja", layered_cols[0], layered_cols[1], outer_cos, outer_sin
    )
    turned_real, turned_imag = rotate(part_real, part_imag, twist_cos, twist_sin)
    freq_real, freq_imag = complex_product(
        "uja,ka->ujk", turned_real, turned_imag, inner_cos, inner_sin
    )
    freq_real = freq_real / PIX
    freq_imag = freq_imag / PIX
    weight = (
        uv_weight[0]
        .astype(jnp.float32)
        .reshape(col_count, inner_count, outer_count)
        .transpose(0, 2, 1)
    )
    visible = (
        gridded_vis[0]
        .astype(jnp.float32)
        .reshape(2, col_count, inner_count, outer_count)
        .transpose(0, 1, 3, 2)
    )
    delta_real = visible[0] - weight * freq_real
    delta_imag = visible[1] - weight * freq_imag
    robust = 1.0 / (1.0 + robust_scale[0] * (delta_real * delta_real + delta_imag * delta_imag))
    weighted_real = robust * delta_real
    weighted_imag = robust * delta_imag
    back_real, back_imag = complex_product(
        "ujk,ak->uja", weighted_real, weighted_imag, inner_cos, -inner_sin
    )
    back_real, back_imag = rotate(back_real, back_imag, twist_cos, -twist_sin)
    back_real, back_imag = complex_product(
        "uja,bj->uba", back_real, back_imag, outer_cos, -outer_sin
    )
    back = jnp.stack([back_real, back_imag]).reshape(2, col_count, slabs, chans, sub)
    back = back.transpose(3, 0, 1, 2, 4).reshape(chans, 2, col_count, slabs * sub)
    back = lax.all_to_all(back, "chan", split_axis=0, concat_axis=0, tiled=True)
    total = jnp.stack(
        [jnp.sum(back * offsets[:, None, None, None] ** t, axis=0) for t in range(TERMS)]
    )
    total = total.reshape(TERMS, 2, col_count, slabs, sub).transpose(3, 1, 2, 0, 4)
    total = total.reshape(slabs, 2, col_count, TERMS * sub)
    total = lax.all_to_all(total, "slab", split_axis=0, concat_axis=0, tiled=True)
    layered_rows = total.transpose(1, 0, 2, 3).reshape(2, inner_count, outer_count, TERMS * sub)
    last_real, last_imag = complex_product(
        "kjy,ak->ajy", layered_rows[0], layered_rows[1], inner_cos, -inner_sin
    )
    last_real, last_imag = rotate(
        last_real, last_imag, twist_cos.T[:, :, None], -twist_sin.T[:, :, None]
    )
    image_out = jnp.einsum("ajy,bj->yba", last_real, outer_cos, precision=HIGHEST) + jnp.einsum(
        "ajy,bj->yba", last_imag, outer_sin, precision=HIGHEST
    )
    image_out = image_out.reshape(TERMS, sub, chans, cols).transpose(2, 0, 1, 3) / PIX
    tiles = lax.all_to_all(image_out, "chan", split_axis=0, concat_axis=0, tiled=True)
    return tiles.transpose(1, 0, 2, 3).reshape(TERMS, rows, cols)


def local(taylor_models, gridded_vis, uv_weight, freq_ratio, robust_scale):
    C, S = lax.axis_size("chan"), lax.axis_size("slab")
    terms, rows, cols = taylor_models.shape
    pix, sub, U = cols * C, rows // C, gridded_vis.shape[2]
    fits = (
        terms == TERMS
        and pix == RADIX * LANES
        and rows * S == pix
        and rows % LANES == 0
        and cols % LANES == 0
        and terms * sub == LANES
        and sub % (8 * PARTS) == 0
        and LANES % (8 * S) == 0
        and U % LANES == 0
    )
    form = tiled if fits else general
    return form(taylor_models, gridded_vis, uv_weight, freq_ratio, robust_scale)


def solution(mesh):
    placed = (
        P(None, "slab", "chan"),
        P("chan", None, "slab", None),
        P("chan", "slab", None),
        P("chan"),
        P("chan"),
    )
    return jax.shard_map(
        local, mesh=mesh, in_specs=placed, out_specs=P(None, "slab", "chan"), check_vma=False
    )
```

profile of v0, /device:TPU:0, one launch (start us, length us, event | category | flops | bytes accessed | tf_op | source)
XLA Modules:
  0.0 165.1 jit_solution(2754833159321773804)
XLA Ops:
  1.3 0.6 broadcast_in_dim.9.freq_ref
  1.9 160.9 %shard_map.91 = f32[2,256,512]{2,1,0:T(8,128)} custom-call(f32[2,256,512]{2,1,0:T(8,128)} %x_hbm.1, bf16[1,2,256,2048]{3,2,1,0:T(8,128)(2,1)} %vis_hbm.1, bf16[1,256,2048]{2,1,0:T(8,128)(2,1)} %wt_hbm.1, f32[8,128]{1,0:T(8,128)} %broadcast_in_dim.9.freq_ref, f32[1]{0:T(128)S(6)} %copy.12.rob_ref, bf16[2,16,256,256]{3,2,1,0:T(8,128)(2,1)} %constant.6.clone.fwd_hbm, ...), custom_call_target="tpu_custom_call" | custom-call | tf_op jit(solution)/shard_map/pallas_call | solution.py:441
  162.8 2.3 %copy.13 = f32[2,256,512]{2,1,0:T(8,128)} copy(f32[2,256,512]{2,1,0:T(8,128)} %shard_map.91) | data formatting | bytes 2097152
where the time goes:
time: 165 us
  Pallas kernels  161 us (98%)
  local copies, waits for them, and re-layouts  2.86 us (2%)
    pallas_call x1, Pallas kernels, tiled(): pl.pallas_call(functools.partial(kernel, C, S), out_shape=jax.ShapeDtypeS...  161 us

commit v1 on v0

--- a/solution.py
+++ b/solution.py
@@ -14,6 +14,9 @@
 RADIX = 16
 LANES = 128
 PARTS = 4
+NEAR, FAR = 0, 1
+BACK_DEPTH = 2
+HALVES = 4
 
 
 def fine_tables():
@@ -23,17 +26,15 @@
     a = np.arange(LANES)[None, None, :]
     angle = 2.0 * np.pi / points * ((a * (RADIX * k + j)) % points)
     cos, sin = np.cos(angle), -np.sin(angle)
-    full = np.concatenate(
-        [np.concatenate([cos, -sin], axis=2), np.concatenate([sin, cos], axis=2)], axis=1
-    ).astype(np.float32)
-    back = np.ascontiguousarray(full.transpose(0, 2, 1))
-
-    def halves(table):
+
+    def halves(real, imag):
+        table = np.concatenate([real, imag], axis=1).astype(np.float32)
         high = table.astype(jnp.bfloat16)
         low = (table - high.astype(np.float32)).astype(jnp.bfloat16)
-        return np.stack([high, low])
-
-    return halves(full), halves(back)
+        return np.concatenate([high, low], axis=2)
+
+    flip = lambda t: t.transpose(0, 2, 1)
+    return halves(cos, sin), halves(flip(cos), -flip(sin))
 
 
 def swap_table(outer, inner):
@@ -101,12 +102,30 @@
     return out
 
 
-def fine(table_ref, j, x):
+def fine(table, x):
     high = x.astype(jnp.bfloat16)
     low = (x - high.astype(jnp.float32)).astype(jnp.bfloat16)
-    t_high, t_low = table_ref[0, j], table_ref[1, j]
-    dot = functools.partial(jnp.dot, preferred_element_type=jnp.float32)
-    return dot(t_high, high) + (dot(t_high, low) + dot(t_low, high))
+    t_high, t_low = table[:, :LANES], table[:, LANES:]
+    left = jnp.concatenate(
+        [jnp.concatenate([t_high, t_high], axis=1), jnp.concatenate([t_low, t_low], axis=1)], axis=0
+    )
+    out = jnp.dot(left, jnp.concatenate([high, low], axis=0), preferred_element_type=jnp.float32)
+    out = out[: 2 * LANES] + out[2 * LANES :]
+    real = out[:LANES, :LANES] - out[LANES:, LANES:]
+    imag = out[:LANES, LANES:] + out[LANES:, :LANES]
+    return real, imag
+
+
+def put(ref, *index, at, value):
+    for part in range(2):
+        v = value[part]
+        if v is None:
+            v = jnp.zeros((8, LANES), jnp.float32)
+        ref[(*index, pl.ds(al8(at), 8), pl.ds(part * LANES, LANES))] = v
+
+
+def get(ref, *index, at):
+    return tuple(ref[(*index, pl.ds(al8(at), 8), pl.ds(part * LANES, LANES))] for part in range(2))
 
 
 def al8(i):
@@ -117,9 +136,9 @@
     C, S,
     x_hbm, vis_hbm, wt_hbm, freq_ref, rob_ref, fwd_hbm, bwd_hbm, pu_hbm, pv_hbm,
     out_hbm,
-    xr, xt, y_s, z_s, w_s, rs, rr, ms, mr, bs, br, ts, tr, x_s, zz_s, os_, fwd, bwd, pu, pv,
+    xr, xt, y_s, z_s, w_s, rs, rr, ms, mr, bs, br, ts, tr, x_s, os_, fwd, bwd, pu, pv,
     raw, vt, offs,
-    load_sem, x_send, x_recv, x_own, o_send, o_recv, o_own, f_send, f_recv,
+    load_sem, x_send, x_recv, x_own, o_send, o_recv, o_own, o_done, f_send, f_recv,
     r_send, r_recv, r_own, m_send, m_recv, m_own, b_send, b_recv, b_own, t_send, t_recv, t_own,
 ):
     H = rs.shape[0]
@@ -131,7 +150,15 @@
     scale = 1.0 / (RADIX * LANES)
     c_me, s_me = lax.axis_index("chan"), lax.axis_index("slab")
     chan_peers = [lax.rem(c_me + d, C) for d in range(1, C)]
-    slab_peers = [lax.rem(s_me + d, S) for d in range(1, S)]
+    if C == 4:
+        chan_peers = [3 - c_me, c_me + 1 - 2 * lax.rem(c_me, 2), lax.rem(c_me + 2, 4)]
+    G = S // 2
+    low = s_me // G * G
+    first_of = (low, G - low)
+    slab_peers = (
+        [low + lax.rem(s_me + d, G) for d in range(1, G)],
+        [G - low + lax.rem(s_me + d, G) for d in range(G)],
+    )
 
     def load(n):
         source, target = (
@@ -156,30 +183,36 @@
     def landed(ref, sem):
         pltpu.make_async_copy(ref, ref, sem).wait()
 
+    half = sub // HALVES
+    halved = lambda p: pl.ds(p * half, half)
+    wide = TERMS * half
+
     barrier = pltpu.get_barrier_semaphore()
-    own(x_hbm.at[:, pl.ds(al8(sub * c_me), sub), :], xr.at[c_me], x_own)
+    for c in chan_peers:
+        pl.semaphore_signal(barrier, inc=1, device_id={"chan": c}, device_id_type=MESH)
+    for s in slab_peers[NEAR] + slab_peers[FAR]:
+        pl.semaphore_signal(barrier, inc=1, device_id={"slab": s}, device_id_type=MESH)
+    for p in range(HALVES):
+        own(
+            x_hbm.at[:, pl.ds(al8(sub * c_me + p * half), half), :],
+            xr.at[c_me, :, halved(p), :], x_own.at[p],
+        )
+    own(freq_ref, offs.at[c_me], o_own)
     for n in range(6):
         load(n).start()
-    for c in chan_peers:
-        pl.semaphore_signal(barrier, inc=1, device_id={"chan": c}, device_id_type=MESH)
-    for s in slab_peers:
-        pl.semaphore_signal(barrier, inc=1, device_id={"slab": s}, device_id_type=MESH)
     pl.semaphore_wait(barrier, C + S - 2)
 
-    for c in chan_peers:
-        remote(
-            x_hbm.at[:, pl.ds(al8(sub * c), sub), :], xr.at[c_me], x_send, x_recv, chan=c
-        )
-    own(freq_ref, offs.at[c_me], o_own)
+    for p in range(HALVES):
+        for c in chan_peers:
+            remote(
+                x_hbm.at[:, pl.ds(al8(sub * c + p * half), half), :],
+                xr.at[c_me, :, halved(p), :], x_send, x_recv.at[p], chan=c,
+            )
     for c in chan_peers:
         remote(freq_ref, offs.at[c_me], f_send, f_recv, chan=c)
 
-    def prep():
-        for n in range(1, 5):
-            load(n).wait()
-
-        def body(n, carry):
-            which, m = n // 8, n % 8
+    def prep(which, first, last):
+        def body(m, carry):
             block = raw[which, :, pl.ds(pl.multiple_of(m * 256, 256), 256)]
             turned = jnp.dot(pu[...], block, preferred_element_type=jnp.float32)
             flipped = lax.dot_general(
@@ -193,63 +226,72 @@
                     ]
             return carry
 
-        lax.fori_loop(0, 24, body, 0)
-
-    def rows_in():
-        landed(xr.at[pl.ds(0, C - 1)], x_recv)
-        landed(xr.at[0], x_own)
-        load(0).wait()
+        lax.fori_loop(first, last, body, 0)
+
+    def rows_in(p):
+        landed(xr.at[pl.ds(0, C - 1), :, halved(p), :], x_recv.at[p])
+        landed(xr.at[0, :, halved(p), :], x_own.at[p])
         per = cols // LANES
         for b in range(RADIX):
-            tile = xr[b // per, :, :, LANES * (b % per) : LANES * (b % per + 1)]
-            xt[b] = tile.reshape(TERMS * sub, LANES).T
+            tile = xr[b // per, :, halved(p), LANES * (b % per) : LANES * (b % per + 1)]
+            xt[b, :, 0:wide] = tile.reshape(wide, LANES).T
 
         def body(n, carry):
-            at = al8(8 * n)
-            out = sixteen([(xt[b, pl.ds(at, 8), :], None) for b in range(RADIX)], -1)
+            out = sixteen([(xt[b, pl.ds(al8(8 * n), 8), :], None) for b in range(RADIX)], -1)
             for j in range(RADIX):
-                for part in range(2):
-                    value = out[j][part]
-                    if value is None:
-                        value = jnp.zeros((8, LANES), jnp.float32)
-                    y_s[j, pl.ds(al8(part * LANES + at), 8), :] = value
+                put(y_s, p, j, at=8 * n, value=out[j])
             return carry
 
         lax.fori_loop(0, LANES // 8, body, 0)
 
-    def rows_out(h):
+    def rows_out(h, p):
         def body(jl, carry):
-            z = fine(fwd, jper * h + jl, y_s[jper * h + jl])
+            z = fine(fwd[jper * h + jl], y_s[p, jper * h + jl])
             for s in range(S):
                 for part in range(2):
-                    w_s[s, part, pl.ds(al8(kl * jl), kl), :] = z[
-                        part * LANES + kl * s : part * LANES + kl * (s + 1), :
-                    ]
-            return carry
-
-        lax.fori_loop(0, jper, body, 0)
+                    w_s[s, part, pl.ds(al8(kl * jl), kl), :] = z[part][kl * s : kl * (s + 1), :]
+            return carry
+
+        lax.fori_loop(0, jper, body, 0, unroll=2)
 
         def flip(s, carry):
             for part in range(2):
-                rs[h, s, part] = w_s[s, part].T.reshape(TERMS, sub, LANES)
+                rs[h, s, part, :, halved(p), :] = w_s[s, part, :, 0:wide].T.reshape(TERMS, half, LANES)
             return carry
 
         lax.fori_loop(0, S, flip, 0)
-        for q in range(PARTS):
-            span = pl.ds(q * piece, piece)
-            own(rs.at[h, s_me, :, :, span, :], rr.at[h, s_me, :, :, span, :], r_own.at[h, q])
-            for s in slab_peers:
-                remote(
-                    rs.at[h, s, :, :, span, :], rr.at[h, s_me, :, :, span, :],
-                    r_send, r_recv.at[h, q], slab=s,
-                )
-
-    def mix(h, q):
+
+    def to_slabs(source, target, g, n, send, recv, done):
+        h, q = n // PARTS, n % PARTS
         span = pl.ds(q * piece, piece)
-        landed(rr.at[h, pl.ds(0, S - 1), :, :, span, :], r_recv.at[h, q])
-        landed(rr.at[h, 0, :, :, span, :], r_own.at[h, q])
-
-        def body(s, carry):
+        for s in slab_peers[g]:
+            remote(
+                source.at[h, s, :, :, span, :], target.at[h, s_me, :, :, span, :],
+                send, recv.at[g, h, q], slab=s,
+            )
+        if g == NEAR:
+            own(
+                source.at[h, s_me, :, :, span, :], target.at[h, s_me, :, :, span, :],
+                done.at[h, q],
+            )
+
+    def from_slabs(target, g, n, recv, done):
+        h, q = n // PARTS, n % PARTS
+        span = pl.ds(q * piece, piece)
+        landed(target.at[h, pl.ds(0, len(slab_peers[g])), :, :, span, :], recv.at[g, h, q])
+        if g == NEAR:
+            landed(target.at[h, 0, :, :, span, :], done.at[h, q])
+
+    def send_rows(g, n):
+        to_slabs(rs, rr, g, n, r_send, r_recv, r_own)
+
+    def mix(g, n):
+        h, q = n // PARTS, n % PARTS
+        span = pl.ds(q * piece, piece)
+        from_slabs(rr, g, n, r_recv, r_own)
+
+        def body(i, carry):
+            s = first_of[g] + i
             base = rr[h, s, :, 0, span, :] * scale
             slope = rr[h, s, :, 1, span, :] * scale
             for c in range(C):
@@ -257,14 +299,15 @@
                 ms[h, c, :, s, span, :] = base + offset[None] * slope
             return carry
 
-        lax.fori_loop(0, S, body, 0)
+        lax.fori_loop(0, G, body, 0)
         there = pl.ds(al8(sub * c_me + q * piece), piece)
-        own(ms.at[h, c_me, :, :, span, :], mr.at[h, :, :, there, :], m_own.at[h])
+        group = pl.ds(first_of[g], G)
         for c in chan_peers:
             remote(
-                ms.at[h, c, :, :, span, :], mr.at[h, :, :, there, :],
+                ms.at[h, c, :, group, span, :], mr.at[h, :, group, there, :],
                 m_send, m_recv.at[h], chan=c,
             )
+        own(ms.at[h, c_me, :, group, span, :], mr.at[h, :, group, there, :], m_own.at[h])
 
     def column_in(h):
         landed(ms.at[h, pl.ds(0, C - 1)], m_recv.at[h])
@@ -278,55 +321,69 @@
                 x.append(tuple(mr[h, part, s, pl.ds(al8(row + at), 8), :] for part in range(2)))
             out = sixteen(x, -1)
             for j in range(RADIX):
-                for part in range(2):
-                    y_s[j, pl.ds(al8(part * LANES + at), 8), :] = out[j][part]
+                put(y_s, h, j, at=at, value=out[j])
             return carry
 
         lax.fori_loop(0, LANES // 8, body, 0)
 
-    def column_mid(h):
+    def column_mid(h, first, last):
         def body(j, carry):
-            z = fine(fwd, j, y_s[j])
+            zr, zi = fine(fwd[j], y_s[h, j])
             weight = vt[2, h, j].astype(jnp.float32)
-            real = vt[0, h, j].astype(jnp.float32) - weight * z[:LANES]
-            imag = vt[1, h, j].astype(jnp.float32) - weight * z[LANES:]
+            real = vt[0, h, j].astype(jnp.float32) - weight * zr
+            imag = vt[1, h, j].astype(jnp.float32) - weight * zi
             robust = 1.0 / (1.0 + rob_ref[0] * (real * real + imag * imag))
-            z_s[j] = fine(bwd, j, jnp.concatenate([robust * real, robust * imag], axis=0))
-            return carry
-
-        lax.fori_loop(0, RADIX, body, 0)
-
-    def column_out(h, q):
-        per = piece // 8
-
+            zr, zi = fine(bwd[j], jnp.concatenate([robust * real, robust * imag], axis=1))
+            z_s[h, j, :, 0:LANES] = zr
+            z_s[h, j, :, LANES : 2 * LANES] = zi
+            return carry
+
+        lax.fori_loop(first, last, body, 0, unroll=2)
+
+    def column_out(h):
         def body(n, carry):
-            at = sub * (n // per) + q * piece + 8 * (n % per)
-            out = sixteen(
-                [tuple(z_s[j, pl.ds(al8(part * LANES + at), 8), :] for part in range(2)) for j in range(RADIX)],
-                1,
-            )
+            out = sixteen([get(z_s, h, j, at=8 * n) for j in range(RADIX)], 1)
             for b in range(RADIX):
                 s, row = LANES * b // rows, LANES * b % rows
                 for part in range(2):
-                    bs[h, part, s, pl.ds(al8(row + at), 8), :] = out[b][part]
-            return carry
-
-        lax.fori_loop(0, LANES // sub * per, body, 0)
+                    bs[h, part, s, pl.ds(al8(row + 8 * n), 8), :] = out[b][part]
+            return carry
+
+        lax.fori_loop(0, LANES // 8, body, 0)
+
+    def send_back(g, n):
+        h, q = n // PARTS, n % PARTS
         span = pl.ds(q * piece, piece)
+        group = pl.ds(first_of[g], G)
         here = lambda c: pl.ds(al8(sub * c + q * piece), piece)
-        own(bs.at[h, :, :, here(c_me), :], br.at[h, c_me, :, :, span, :], b_own.at[h, q])
         for c in chan_peers:
             remote(
-                bs.at[h, :, :, here(c), :], br.at[h, c_me, :, :, span, :],
-                b_send, b_recv.at[h, q], chan=c,
+                bs.at[h, :, group, here(c), :], br.at[h, c_me, :, group, span, :],
+                b_send, b_recv.at[g, h, q], chan=c,
             )
-
-    def gather(h, q):
+        own(
+            bs.at[h, :, group, here(c_me), :], br.at[h, c_me, :, group, span, :],
+            b_own.at[g, h, q],
+        )
+
+    arrived = set()
+
+    def returned(g, n):
+        if (g, n) not in arrived:
+            arrived.add((g, n))
+            from_slabs(tr, g, n, t_recv, t_own)
+
+    def gather(g, n):
+        h, q = n // PARTS, n % PARTS
         span = pl.ds(q * piece, piece)
-        landed(br.at[h, pl.ds(0, C - 1), :, :, span, :], b_recv.at[h, q])
-        landed(br.at[h, 0, :, :, span, :], b_own.at[h, q])
-
-        def body(s, carry):
+        group = pl.ds(first_of[g], G)
+        if g == FAR and n >= BACK_DEPTH:
+            returned(g, n - BACK_DEPTH)
+        landed(br.at[h, pl.ds(0, C - 1), :, group, span, :], b_recv.at[g, h, q])
+        landed(br.at[h, 0, :, group, span, :], b_own.at[g, h, q])
+
+        def body(i, carry):
+            s = first_of[g] + i
             base, slope = None, None
             for c in range(C):
                 offset = (offs[c, 0:1, :] - 1.0)[None]
@@ -337,23 +394,18 @@
             ts[h, s, :, 1, span, :] = slope * scale
             return carry
 
-        lax.fori_loop(0, S, body, 0)
-        own(ts.at[h, s_me, :, :, span, :], tr.at[h, s_me, :, :, span, :], t_own.at[h])
-        for s in slab_peers:
-            remote(
-                ts.at[h, s, :, :, span, :], tr.at[h, s_me, :, :, span, :],
-                t_send, t_recv.at[h], slab=s,
-            )
-
-    def back_in(h):
-        landed(tr.at[h, pl.ds(0, S - 1)], t_recv.at[h])
-        landed(tr.at[h, 0], t_own.at[h])
+        lax.fori_loop(0, G, body, 0)
+        to_slabs(ts, tr, g, n, t_send, t_recv, t_own)
+
+    def back_in(h, p):
+        returned(FAR, h * PARTS + p)
+        returned(NEAR, h * PARTS + p)
 
         def flip(s, carry):
             for part in range(2):
-                tile = tr[h, s, part].reshape(TERMS * sub, LANES).T
+                tile = tr[h, s, part, :, halved(p), :].reshape(wide, LANES).T
                 for jl in range(jper):
-                    x_s[jper * h + jl, pl.ds(al8(part * LANES + kl * s), kl), :] = tile[
+                    x_s[jl, pl.ds(al8(kl * s), kl), part * LANES : part * LANES + wide] = tile[
                         kl * jl : kl * (jl + 1), :
                     ]
             return carry
@@ -361,54 +413,139 @@
         lax.fori_loop(0, S, flip, 0)
 
         def body(jl, carry):
-            zz_s[jper * h + jl] = fine(bwd, jper * h + jl, x_s[jper * h + jl])
-            return carry
-
-        lax.fori_loop(0, jper, body, 0)
-
-    def back_out():
+            zr, zi = fine(bwd[jper * h + jl], x_s[jl])
+            y_s[p, jper * h + jl, :, 0:LANES] = zr
+            y_s[p, jper * h + jl, :, LANES : 2 * LANES] = zi
+            return carry
+
+        lax.fori_loop(0, jper, body, 0, unroll=2)
+
+    def back_out(p):
         def body(n, carry):
-            at = 8 * n
-            out = sixteen(
-                [tuple(zz_s[j, pl.ds(al8(part * LANES + at), 8), :] for part in range(2)) for j in range(RADIX)],
-                1,
-            )
+            out = sixteen([get(y_s, p, j, at=8 * n) for j in range(RADIX)], 1)
             for b in range(RADIX):
-                xt[b, pl.ds(al8(at), 8), :] = out[b][0]
+                xt[b, pl.ds(al8(8 * n), 8), :] = out[b][0]
             return carry
 
         lax.fori_loop(0, LANES // 8, body, 0)
         per = cols // LANES
         for b in range(RADIX):
-            os_[b // per, :, :, LANES * (b % per) : LANES * (b % per + 1)] = xt[b].T.reshape(
-                TERMS, sub, LANES
+            os_[b // per, :, halved(p), LANES * (b % per) : LANES * (b % per + 1)] = (
+                xt[b, :, 0:wide].T.reshape(TERMS, half, LANES)
             )
-        there = pl.ds(al8(sub * c_me), sub)
+        there = pl.ds(al8(sub * c_me + p * half), half)
         for c in chan_peers:
-            remote(os_.at[c], out_hbm.at[:, there, :], o_send, o_recv, chan=c)
-        own(os_.at[c_me], out_hbm.at[:, there, :], o_own)
-
-    prep()
+            remote(os_.at[c, :, halved(p), :], out_hbm.at[:, there, :], o_send, o_recv, chan=c)
+        own(os_.at[c_me, :, halved(p), :], out_hbm.at[:, there, :], o_done)
+
+    for n in range(1, 5):
+        load(n).wait()
+    prep(0, 0, 8)
+    load(0).wait()
+    load(5).wait()
+    landed(offs.at[0], o_own)
+    rows_in(0)
+    rows_out(0, 0)
+    send_rows(FAR, 0)
+    send_rows(NEAR, 0)
+    rows_in(1)
+    rows_out(0, 1)
+    send_rows(FAR, 1)
+    send_rows(NEAR, 1)
     landed(offs.at[pl.ds(0, C - 1)], f_recv)
-    landed(offs.at[0], o_own)
-    rows_in()
-    for h in range(H):
-        rows_out(h)
-    for h in range(H):
-        for q in range(PARTS):
-            mix(h, q)
-    load(5).wait()
-    for h in range(H):
-        column_in(h)
-        column_mid(h)
-        for q in range(PARTS):
-            column_out(h, q)
-    for h in range(H):
-        for q in range(PARTS):
-            gather(h, q)
-    for h in range(H):
-        back_in(h)
-    back_out()
+    mix(NEAR, 0)
+    rows_in(2)
+    rows_out(0, 2)
+    send_rows(NEAR, 2)
+    mix(NEAR, 1)
+    mix(FAR, 0)
+    send_rows(FAR, 2)
+    rows_in(3)
+    rows_out(0, 3)
+    send_rows(NEAR, 3)
+    mix(NEAR, 2)
+    rows_out(1, 0)
+    mix(NEAR, 3)
+    mix(FAR, 1)
+    send_rows(FAR, 3)
+    rows_out(1, 1)
+    prep(1, 0, 4)
+    mix(FAR, 2)
+    send_rows(FAR, 4)
+    send_rows(NEAR, 4)
+    prep(1, 4, 8)
+    rows_out(1, 2)
+    mix(FAR, 3)
+    send_rows(FAR, 5)
+    send_rows(NEAR, 5)
+    rows_out(1, 3)
+    mix(NEAR, 4)
+    prep(2, 0, 4)
+    mix(NEAR, 5)
+    mix(FAR, 4)
+    send_rows(FAR, 6)
+    send_rows(NEAR, 6)
+    prep(2, 4, 8)
+    column_in(0)
+    mix(NEAR, 6)
+    column_mid(0, 0, 4)
+    mix(FAR, 5)
+    send_rows(FAR, 7)
+    send_rows(NEAR, 7)
+    column_mid(0, 4, 10)
+    mix(NEAR, 7)
+    column_mid(0, 10, 16)
+    column_out(0)
+    send_back(FAR, 0)
+    mix(FAR, 6)
+    send_back(FAR, 1)
+    mix(FAR, 7)
+    send_back(FAR, 2)
+    gather(FAR, 0)
+    send_back(FAR, 3)
+    gather(FAR, 1)
+    send_back(NEAR, 0)
+    column_in(1)
+    send_back(NEAR, 1)
+    column_mid(1, 0, 8)
+    gather(FAR, 2)
+    column_mid(1, 8, 16)
+    gather(FAR, 3)
+    column_out(1)
+    send_back(FAR, 4)
+    gather(NEAR, 0)
+    send_back(FAR, 5)
+    gather(NEAR, 1)
+    send_back(FAR, 6)
+    send_back(FAR, 7)
+    gather(FAR, 4)
+    send_back(NEAR, 2)
+    gather(FAR, 5)
+    send_back(NEAR, 3)
+    back_in(0, 0)
+    gather(FAR, 6)
+    send_back(NEAR, 4)
+    back_in(0, 1)
+    gather(FAR, 7)
+    send_back(NEAR, 5)
+    gather(NEAR, 2)
+    send_back(NEAR, 6)
+    gather(NEAR, 3)
+    send_back(NEAR, 7)
+    gather(NEAR, 4)
+    back_in(0, 2)
+    gather(NEAR, 5)
+    back_in(0, 3)
+    gather(NEAR, 6)
+    back_in(1, 0)
+    back_out(0)
+    gather(NEAR, 7)
+    back_in(1, 1)
+    back_out(1)
+    back_in(1, 2)
+    back_out(2)
+    back_in(1, 3)
+    back_out(3)
 
     landed(xr.at[pl.ds(0, C - 1)], x_send)
     landed(offs.at[pl.ds(0, C - 1)], f_send)
@@ -418,7 +555,7 @@
     landed(ts.at[:, pl.ds(0, S - 1)], t_send)
     landed(os_.at[pl.ds(0, C - 1)], o_send)
     landed(os_.at[pl.ds(0, C - 1)], o_recv)
-    landed(os_.at[0], o_own)
+    landed(os_.at[0], o_done)
 
 
 def tiled(taylor_models, gridded_vis, uv_weight, freq_ratio, robust_scale):
@@ -431,7 +568,7 @@
     pu, pv = swap_table(RADIX, U // RADIX), swap_table(RADIX, 16)
     freq = jnp.broadcast_to(freq_ratio[:, None], (8, LANES))
     f32, bf16 = jnp.float32, jnp.bfloat16
-    stage = (RADIX, 2 * LANES, LANES)
+    stage = (RADIX, LANES, 2 * LANES)
     slabbed = (H, S, 2, terms, sub, LANES)
     chanbed = (H, C, 2, S, sub, LANES)
     natural = (H, 2, S, rows, LANES)
@@ -448,18 +585,18 @@
         ],
         out_specs=anywhere,
         scratch_shapes=[
-            V((C, terms, sub, cols)), V((RADIX, LANES, LANES)), V(stage), V(stage),
+            V((C, terms, sub, cols)), V((RADIX, LANES, LANES)), V((HALVES, *stage)), V((H, *stage)),
             V((S, 2, LANES, LANES)), V(slabbed), V(slabbed), V(chanbed), V(natural),
-            V(natural), V(chanbed), V(slabbed), V(slabbed), V(stage), V(stage),
+            V(natural), V(chanbed), V(slabbed), V(slabbed), V(stage),
             V((C, terms, sub, cols)), V(fwd.shape, bf16), V(bwd.shape, bf16),
             V(pu.shape, bf16), V(pv.shape, bf16),
             V((3, U, RADIX * LANES), bf16), V((3, H, RADIX, LANES, LANES), bf16),
             V((C, 8, LANES)),
-            D((6,)), D(()), D(()), D(()), D(()), D(()), D(()), D(()), D(()),
-            D(()), D((H, PARTS)), D((H, PARTS)),
+            D((6,)), D(()), D((HALVES,)), D((HALVES,)), D(()), D(()), D(()), D(()), D(()), D(()),
+            D(()), D((2, H, PARTS)), D((H, PARTS)),
             D(()), D((H,)), D((H,)),
-            D(()), D((H, PARTS)), D((H, PARTS)),
-            D(()), D((H,)), D((H,)),
+            D(()), D((2, H, PARTS)), D((2, H, PARTS)),
+            D(()), D((2, H, PARTS)), D((H, PARTS)),
         ],
         compiler_params=pltpu.CompilerParams(
             collective_id=0, has_side_effects=True, vmem_limit_bytes=63 * 1024 * 1024
@@ -611,7 +748,9 @@
         and terms * sub == LANES
         and sub % (8 * PARTS) == 0
         and LANES % (8 * S) == 0
-        and U % LANES == 0
+        and S % 2 == 0
+        and PARTS == HALVES
+        and U == 2 * LANES
     )
     form = tiled if fits else general
     return form(taylor_models, gridded_vis, uv_weight, freq_ratio, robust_scale)

time: 165 us -> 139 us (0.84)
  Pallas kernels: 161 us -> 135 us
    pallas_call x1, Pallas kernels: 161 us -> 135 us  [tiled(): pl.pallas_call(functools.partial(kernel, C, S), out_shape=jax.ShapeDtypeS...]
where the time goes in v1:
time: 139 us
  Pallas kernels  135 us (97%)
  local copies, waits for them, and re-layouts  2.86 us (2%)
    pallas_call x1, Pallas kernels, tiled(): pl.pallas_call(functools.partial(kernel, C, S), out_shape=jax.ShapeDtypeS...  135 us

profile of v1, /device:TPU:0, one launch (start us, length us, event | category | flops | bytes accessed | tf_op | source)
XLA Modules:
  0.0 139.1 jit_solution(7755575922347182938)
XLA Ops:
  1.3 0.6 broadcast_in_dim.9.freq_ref
  1.9 134.9 %shard_map.91 = f32[2,256,512]{2,1,0:T(8,128)} custom-call(f32[2,256,512]{2,1,0:T(8,128)} %x_hbm.1, bf16[1,2,256,2048]{3,2,1,0:T(8,128)(2,1)} %vis_hbm.1, bf16[1,256,2048]{2,1,0:T(8,128)(2,1)} %wt_hbm.1, f32[8,128]{1,0:T(8,128)} %broadcast_in_dim.9.freq_ref, f32[1]{0:T(128)S(6)} %copy.12.rob_ref, bf16[16,256,256]{2,1,0:T(8,128)(2,1)} %constant.6.clone.fwd_hbm, ...), custom_call_target="tpu_custom_call" | custom-call | tf_op jit(solution)/shard_map/pallas_call | solution.py:578
  136.8 2.3 %copy.13 = f32[2,256,512]{2,1,0:T(8,128)} copy(f32[2,256,512]{2,1,0:T(8,128)} %shard_map.91) | data formatting | bytes 2097152

commit v2 on v1

--- a/solution.py
+++ b/solution.py
@@ -15,7 +15,7 @@
 LANES = 128
 PARTS = 4
 NEAR, FAR = 0, 1
-BACK_DEPTH = 2
+BACK_DEPTH = 8
 HALVES = 4
 
 
@@ -111,8 +111,9 @@
     )
     out = jnp.dot(left, jnp.concatenate([high, low], axis=0), preferred_element_type=jnp.float32)
     out = out[: 2 * LANES] + out[2 * LANES :]
-    real = out[:LANES, :LANES] - out[LANES:, LANES:]
-    imag = out[:LANES, LANES:] + out[LANES:, :LANES]
+    n = x.shape[1] // 2
+    real = out[:LANES, :n] - out[LANES:, n:]
+    imag = out[:LANES, n:] + out[LANES:, :n]
     return real, imag
 
 
@@ -137,7 +138,7 @@
     x_hbm, vis_hbm, wt_hbm, freq_ref, rob_ref, fwd_hbm, bwd_hbm, pu_hbm, pv_hbm,
     out_hbm,
     xr, xt, y_s, z_s, w_s, rs, rr, ms, mr, bs, br, ts, tr, x_s, os_, fwd, bwd, pu, pv,
-    raw, vt, offs,
+    raw, vt, offs, mine,
     load_sem, x_send, x_recv, x_own, o_send, o_recv, o_own, o_done, f_send, f_recv,
     r_send, r_recv, r_own, m_send, m_recv, m_own, b_send, b_recv, b_own, t_send, t_recv, t_own,
 ):
@@ -187,6 +188,7 @@
     halved = lambda p: pl.ds(p * half, half)
     wide = TERMS * half
 
+    mine[...] = jnp.full(mine.shape, freq_ref[0] - 1.0, jnp.float32)
     barrier = pltpu.get_barrier_semaphore()
     for c in chan_peers:
         pl.semaphore_signal(barrier, inc=1, device_id={"chan": c}, device_id_type=MESH)
@@ -197,19 +199,20 @@
             x_hbm.at[:, pl.ds(al8(sub * c_me + p * half), half), :],
             xr.at[c_me, :, halved(p), :], x_own.at[p],
         )
-    own(freq_ref, offs.at[c_me], o_own)
     for n in range(6):
         load(n).start()
     pl.semaphore_wait(barrier, C + S - 2)
 
-    for p in range(HALVES):
+    own(mine, offs.at[c_me], o_own)
+    for c in chan_peers:
+        remote(mine, offs.at[c_me], f_send, f_recv, chan=c)
+
+    def send_tiles(p):
         for c in chan_peers:
             remote(
                 x_hbm.at[:, pl.ds(al8(sub * c + p * half), half), :],
                 xr.at[c_me, :, halved(p), :], x_send, x_recv.at[p], chan=c,
             )
-    for c in chan_peers:
-        remote(freq_ref, offs.at[c_me], f_send, f_recv, chan=c)
 
     def prep(which, first, last):
         def body(m, carry):
@@ -252,14 +255,14 @@
                     w_s[s, part, pl.ds(al8(kl * jl), kl), :] = z[part][kl * s : kl * (s + 1), :]
             return carry
 
-        lax.fori_loop(0, jper, body, 0, unroll=2)
+        lax.fori_loop(0, jper, body, 0, unroll=4)
 
         def flip(s, carry):
             for part in range(2):
                 rs[h, s, part, :, halved(p), :] = w_s[s, part, :, 0:wide].T.reshape(TERMS, half, LANES)
             return carry
 
-        lax.fori_loop(0, S, flip, 0)
+        lax.fori_loop(0, S, flip, 0, unroll=2)
 
     def to_slabs(source, target, g, n, send, recv, done):
         h, q = n // PARTS, n % PARTS
@@ -295,7 +298,7 @@
             base = rr[h, s, :, 0, span, :] * scale
             slope = rr[h, s, :, 1, span, :] * scale
             for c in range(C):
-                offset = offs[c, 0:1, :] - 1.0
+                offset = offs[c, 0:1, :]
                 ms[h, c, :, s, span, :] = base + offset[None] * slope
             return carry
 
@@ -386,7 +389,7 @@
             s = first_of[g] + i
             base, slope = None, None
             for c in range(C):
-                offset = (offs[c, 0:1, :] - 1.0)[None]
+                offset = (offs[c, 0:1, :])[None]
                 value = br[h, c, :, s, span, :]
                 base = value if base is None else base + value
                 slope = offset * value if slope is None else slope + offset * value
@@ -410,7 +413,7 @@
                     ]
             return carry
 
-        lax.fori_loop(0, S, flip, 0)
+        lax.fori_loop(0, S, flip, 0, unroll=2)
 
         def body(jl, carry):
             zr, zi = fine(bwd[jper * h + jl], x_s[jl])
@@ -418,7 +421,7 @@
             y_s[p, jper * h + jl, :, LANES : 2 * LANES] = zi
             return carry
 
-        lax.fori_loop(0, jper, body, 0, unroll=2)
+        lax.fori_loop(0, jper, body, 0, unroll=4)
 
     def back_out(p):
         def body(n, carry):
@@ -438,6 +441,8 @@
             remote(os_.at[c, :, halved(p), :], out_hbm.at[:, there, :], o_send, o_recv, chan=c)
         own(os_.at[c_me, :, halved(p), :], out_hbm.at[:, there, :], o_done)
 
+    for p in range(HALVES):
+        send_tiles(p)
     for n in range(1, 5):
         load(n).wait()
     prep(0, 0, 8)
@@ -446,104 +451,103 @@
     landed(offs.at[0], o_own)
     rows_in(0)
     rows_out(0, 0)
+    send_rows(NEAR, 0)
     send_rows(FAR, 0)
-    send_rows(NEAR, 0)
     rows_in(1)
     rows_out(0, 1)
+    send_rows(NEAR, 1)
     send_rows(FAR, 1)
-    send_rows(NEAR, 1)
     landed(offs.at[pl.ds(0, C - 1)], f_recv)
     mix(NEAR, 0)
     rows_in(2)
     rows_out(0, 2)
     send_rows(NEAR, 2)
     mix(NEAR, 1)
-    mix(FAR, 0)
-    send_rows(FAR, 2)
     rows_in(3)
     rows_out(0, 3)
     send_rows(NEAR, 3)
+    mix(FAR, 0)
+    send_rows(FAR, 2)
     mix(NEAR, 2)
     rows_out(1, 0)
     mix(NEAR, 3)
+    prep(1, 0, 4)
     mix(FAR, 1)
     send_rows(FAR, 3)
     rows_out(1, 1)
-    prep(1, 0, 4)
-    mix(FAR, 2)
-    send_rows(FAR, 4)
-    send_rows(NEAR, 4)
     prep(1, 4, 8)
     rows_out(1, 2)
+    mix(FAR, 2)
+    send_rows(NEAR, 4)
+    send_rows(FAR, 4)
+    rows_out(1, 3)
+    prep(2, 0, 4)
     mix(FAR, 3)
+    send_rows(NEAR, 5)
     send_rows(FAR, 5)
-    send_rows(NEAR, 5)
-    rows_out(1, 3)
     mix(NEAR, 4)
-    prep(2, 0, 4)
+    prep(2, 4, 8)
     mix(NEAR, 5)
+    column_in(0)
     mix(FAR, 4)
+    send_rows(NEAR, 6)
     send_rows(FAR, 6)
-    send_rows(NEAR, 6)
-    prep(2, 4, 8)
-    column_in(0)
-    mix(NEAR, 6)
-    column_mid(0, 0, 4)
+    column_mid(0, 0, 10)
     mix(FAR, 5)
+    send_rows(NEAR, 7)
     send_rows(FAR, 7)
-    send_rows(NEAR, 7)
-    column_mid(0, 4, 10)
-    mix(NEAR, 7)
     column_mid(0, 10, 16)
     column_out(0)
     send_back(FAR, 0)
+    mix(NEAR, 6)
+    send_back(FAR, 1)
     mix(FAR, 6)
-    send_back(FAR, 1)
+    send_back(FAR, 2)
+    mix(NEAR, 7)
+    gather(FAR, 0)
     mix(FAR, 7)
-    send_back(FAR, 2)
-    gather(FAR, 0)
     send_back(FAR, 3)
     gather(FAR, 1)
     send_back(NEAR, 0)
+    gather(FAR, 2)
+    send_back(NEAR, 1)
     column_in(1)
-    send_back(NEAR, 1)
     column_mid(1, 0, 8)
-    gather(FAR, 2)
+    gather(FAR, 3)
     column_mid(1, 8, 16)
-    gather(FAR, 3)
     column_out(1)
     send_back(FAR, 4)
+    send_back(FAR, 5)
     gather(NEAR, 0)
-    send_back(FAR, 5)
     gather(NEAR, 1)
     send_back(FAR, 6)
     send_back(FAR, 7)
     gather(FAR, 4)
+    send_back(NEAR, 4)
+    gather(FAR, 5)
+    send_back(NEAR, 5)
+    back_in(0, 0)
     send_back(NEAR, 2)
-    gather(FAR, 5)
-    send_back(NEAR, 3)
-    back_in(0, 0)
     gather(FAR, 6)
-    send_back(NEAR, 4)
+    send_back(NEAR, 6)
     back_in(0, 1)
     gather(FAR, 7)
-    send_back(NEAR, 5)
-    gather(NEAR, 2)
-    send_back(NEAR, 6)
-    gather(NEAR, 3)
+    send_back(NEAR, 3)
     send_back(NEAR, 7)
     gather(NEAR, 4)
-    back_in(0, 2)
     gather(NEAR, 5)
-    back_in(0, 3)
-    gather(NEAR, 6)
     back_in(1, 0)
     back_out(0)
-    gather(NEAR, 7)
+    gather(NEAR, 2)
     back_in(1, 1)
     back_out(1)
+    gather(NEAR, 6)
+    back_in(0, 2)
+    gather(NEAR, 3)
     back_in(1, 2)
     back_out(2)
+    gather(NEAR, 7)
+    back_in(0, 3)
     back_in(1, 3)
     back_out(3)
 
@@ -566,7 +570,6 @@
     H = U // LANES
     fwd, bwd = fine_tables()
     pu, pv = swap_table(RADIX, U // RADIX), swap_table(RADIX, 16)
-    freq = jnp.broadcast_to(freq_ratio[:, None], (8, LANES))
     f32, bf16 = jnp.float32, jnp.bfloat16
     stage = (RADIX, LANES, 2 * LANES)
     slabbed = (H, S, 2, terms, sub, LANES)
@@ -580,18 +583,18 @@
         out_shape=jax.ShapeDtypeStruct(taylor_models.shape, f32),
         in_specs=[
             anywhere, anywhere, anywhere,
-            pl.BlockSpec(memory_space=pltpu.VMEM), pl.BlockSpec(memory_space=pltpu.SMEM),
+            pl.BlockSpec(memory_space=pltpu.SMEM), pl.BlockSpec(memory_space=pltpu.SMEM),
             anywhere, anywhere, anywhere, anywhere,
         ],
         out_specs=anywhere,
         scratch_shapes=[
             V((C, terms, sub, cols)), V((RADIX, LANES, LANES)), V((HALVES, *stage)), V((H, *stage)),
             V((S, 2, LANES, LANES)), V(slabbed), V(slabbed), V(chanbed), V(natural),
-            V(natural), V(chanbed), V(slabbed), V(slabbed), V(stage),
+            V(natural), V(chanbed), V(slabbed), V(slabbed), V((RADIX // H, LANES, 2 * LANES)),
             V((C, terms, sub, cols)), V(fwd.shape, bf16), V(bwd.shape, bf16),
             V(pu.shape, bf16), V(pv.shape, bf16),
             V((3, U, RADIX * LANES), bf16), V((3, H, RADIX, LANES, LANES), bf16),
-            V((C, 8, LANES)),
+            V((C, 8, LANES)), V((8, LANES)),
             D((6,)), D(()), D((HALVES,)), D((HALVES,)), D(()), D(()), D(()), D(()), D(()), D(()),
             D(()), D((2, H, PARTS)), D((H, PARTS)),
             D(()), D((H,)), D((H,)),
@@ -601,7 +604,7 @@
         compiler_params=pltpu.CompilerParams(
             collective_id=0, has_side_effects=True, vmem_limit_bytes=63 * 1024 * 1024
         ),
-    )(taylor_models, gridded_vis, uv_weight, freq, robust_scale, fwd, bwd, pu, pv)
+    )(taylor_models, gridded_vis, uv_weight, freq_ratio, robust_scale, fwd, bwd, pu, pv)
 
 
 HIGHEST = lax.Precision.HIGH

time: 139 us -> 130 us (0.935)
  Pallas kernels: 135 us -> 126 us
    pallas_call x1, Pallas kernels: 135 us -> 126 us  [tiled(): pl.pallas_call(functools.partial(kernel, C, S), out_shape=jax.ShapeDtypeS...]
where the time goes in v2:
time: 130 us; the launch traced here: 129 us
  Pallas kernels  126 us (97%)
  local copies, waits for them, and re-layouts  2.26 us (2%)
  between operations  1.3 us (1%)
    pallas_call x1, Pallas kernels, tiled(): pl.pallas_call(functools.partial(kernel, C, S), out_shape=jax.ShapeDtypeS...  126 us

profile of v2, /device:TPU:0, one launch (start us, length us, event | category | flops | bytes accessed | tf_op | source)
XLA Modules:
  0.0 129.3 jit_solution(4865040552712664007)
XLA Ops:
  1.3 125.8 %shard_map.91 = f32[2,256,512]{2,1,0:T(8,128)} custom-call(f32[2,256,512]{2,1,0:T(8,128)} %x_hbm.1, bf16[1,2,256,2048]{3,2,1,0:T(8,128)(2,1)} %vis_hbm.1, bf16[1,256,2048]{2,1,0:T(8,128)(2,1)} %wt_hbm.1, f32[1]{0:T(128)S(6)} %copy.11.freq_ref, f32[1]{0:T(128)S(6)} %copy.12.rob_ref, bf16[16,256,256]{2,1,0:T(8,128)(2,1)} %constant.6.clone.fwd_hbm, ...), custom_call_target="tpu_custom_call" | custom-call | tf_op jit(solution)/shard_map/pallas_call | solution.py:581
  127.1 2.3 %copy.13 = f32[2,256,512]{2,1,0:T(8,128)} copy(f32[2,256,512]{2,1,0:T(8,128)} %shard_map.91) | data formatting | bytes 2097152

commit v3 on v2

--- a/solution.py
+++ b/solution.py
@@ -15,7 +15,6 @@
 LANES = 128
 PARTS = 4
 NEAR, FAR = 0, 1
-BACK_DEPTH = 8
 HALVES = 4
 
 
@@ -341,7 +340,7 @@
             z_s[h, j, :, LANES : 2 * LANES] = zi
             return carry
 
-        lax.fori_loop(first, last, body, 0, unroll=2)
+        lax.fori_loop(first, last, body, 0, unroll=4)
 
     def column_out(h):
         def body(n, carry):
@@ -380,8 +379,6 @@
         h, q = n // PARTS, n % PARTS
         span = pl.ds(q * piece, piece)
         group = pl.ds(first_of[g], G)
-        if g == FAR and n >= BACK_DEPTH:
-            returned(g, n - BACK_DEPTH)
         landed(br.at[h, pl.ds(0, C - 1), :, group, span, :], b_recv.at[g, h, q])
         landed(br.at[h, 0, :, group, span, :], b_own.at[g, h, q])
 
@@ -393,8 +390,8 @@
                 value = br[h, c, :, s, span, :]
                 base = value if base is None else base + value
                 slope = offset * value if slope is None else slope + offset * value
-            ts[h, s, :, 0, span, :] = base * scale
-            ts[h, s, :, 1, span, :] = slope * scale
+            ts[h, s, :, 0, span, :] = base
+            ts[h, s, :, 1, span, :] = slope
             return carry
 
         lax.fori_loop(0, G, body, 0)
@@ -492,11 +489,11 @@
     mix(FAR, 4)
     send_rows(NEAR, 6)
     send_rows(FAR, 6)
-    column_mid(0, 0, 10)
+    column_mid(0, 0, 8)
     mix(FAR, 5)
     send_rows(NEAR, 7)
     send_rows(FAR, 7)
-    column_mid(0, 10, 16)
+    column_mid(0, 8, 16)
     column_out(0)
     send_back(FAR, 0)
     mix(NEAR, 6)
@@ -517,9 +514,9 @@
     column_mid(1, 8, 16)
     column_out(1)
     send_back(FAR, 4)
-    send_back(FAR, 5)
     gather(NEAR, 0)
     gather(NEAR, 1)
+    send_back(FAR, 5)
     send_back(FAR, 6)
     send_back(FAR, 7)
     gather(FAR, 4)
@@ -578,7 +575,7 @@
     V = lambda shape, dtype=f32: pltpu.VMEM(shape, dtype)
     D = pltpu.SemaphoreType.DMA
     anywhere = pl.BlockSpec(memory_space=pl.ANY)
-    return pl.pallas_call(
+    image = pl.pallas_call(
         functools.partial(kernel, C, S),
         out_shape=jax.ShapeDtypeStruct(taylor_models.shape, f32),
         in_specs=[
@@ -605,6 +602,7 @@
             collective_id=0, has_side_effects=True, vmem_limit_bytes=63 * 1024 * 1024
         ),
     )(taylor_models, gridded_vis, uv_weight, freq_ratio, robust_scale, fwd, bwd, pu, pv)
+    return image * (1.0 / (RADIX * LANES))
 
 
 HIGHEST = lax.Precision.HIGH

time: 130 us -> 129 us (level)
  other arithmetic: 0 us -> 2.29 us
  local copies, waits for them, and re-layouts: 2.26 us -> 0 us
    mul x0 -> x1, other arithmetic: none -> 2.29 us  [tiled(): return image * (1.0 / (RADIX * LANES))]
    unnamed x1 -> x0, local copies, waits for them, and re-layouts: 2.26 us -> none
where the time goes in v3:
time: 129 us
  Pallas kernels  125 us (97%)
  other arithmetic  2.29 us (2%)
  between operations  1.3 us (1%)
    pallas_call x1, Pallas kernels, tiled(): pl.pallas_call(functools.partial(kernel, C, S), out_shape=jax.ShapeDtypeS...  125 us

profile of v3, /device:TPU:0, one launch (start us, length us, event | category | flops | bytes accessed | tf_op | source)
XLA Modules:
  0.0 128.7 jit_solution(7689674731654308295)
XLA Ops:
  1.3 125.1 %shard_map.91 = f32[2,256,512]{2,1,0:T(8,128)} custom-call(f32[2,256,512]{2,1,0:T(8,128)} %x_hbm.1, bf16[1,2,256,2048]{3,2,1,0:T(8,128)(2,1)} %vis_hbm.1, bf16[1,256,2048]{2,1,0:T(8,128)(2,1)} %wt_hbm.1, f32[1]{0:T(128)S(6)} %copy.10.freq_ref, f32[1]{0:T(128)S(6)} %copy.11.rob_ref, bf16[16,256,256]{2,1,0:T(8,128)(2,1)} %constant.8.clone.fwd_hbm, ...), custom_call_target="tpu_custom_call" | custom-call | tf_op jit(solution)/shard_map/pallas_call | solution.py:578
  126.4 2.3 %broadcast_multiply_fusion = f32[2,256,512]{2,1,0:T(8,128)} fusion(f32[2,256,512]{2,1,0:T(8,128)} %shard_map.91), kind=kLoop, calls=%fused_computation | loop fusion | flops 262144 | bytes 2097152 | tf_op jit(solution)/shard_map/mul | solution.py:605
